TPU v7x, 1024 devices: a whole 4x8x16 slice. The times are simulated.
1024 devices in a mesh: expert: 64 (over z, x_hi, core), mp: 16 (over y, x_lo).
Axes of the slice: x: 4 (x_hi: 2, x_lo: 2; x = x_hi * 2 + x_lo), y: 8, z: 16, core: 2. Of those that a mesh axis runs over, the one named last changes fastest.
Arguments:
- tokens: bfloat16 [2, 20480, 2048], P(None, 'expert', 'mp'), may hold values from -6 to 6
- expert_index: int32 [2, 20480], P(None, 'expert'), may hold values from 0 to 63
- slot_index: int32 [2, 20480], P(None, 'expert'), may hold values from 0 to 5, as said below
- kept_mask: int32 [2, 20480], P(None, 'expert'), may hold values from 0 to 1
- gate_prob: float32 [2, 20480], P(None, 'expert'), may hold values from 0.2 to 1
- w_in: bfloat16 [64, 2048, 6144], P('expert', None, 'mp'), may hold values from -0.125 to 0.125
- w_out: bfloat16 [64, 6144, 2048], P('expert', 'mp'), may hold values from -0.078125 to 0.078125
Outputs:
- mixed: bfloat16 [2, 20480, 2048], P(None, 'expert', 'mp')
Inputs may be any that keep to these rules, and one draw needn't show every extreme that they name: `slot_index`: within one aligned block of 320 tokens of a group, no two kept tokens share both expert and slot; in every group some expert has all 6 slots of every block taken. Dropped tokens carry a slot value too, which means nothing.
All inputs are finite; a program needn't handle non-finite values.
Results may differ from a plain program's by a relative error of at most 0.018.
Values may be sent and summed in bfloat16 or wider, within the bound.
A program may use at most 32 MiB of HBM per device.

v0:
```python
import jax
import jax.numpy as jnp
from jax import lax
from jax.sharding import Mesh
from jax.sharding import PartitionSpec as P

GROUPS = 2
CAP = 6
EXPERT = ("expert_0", "expert_1", "expert_2")
MP = ("mp_0", "mp_1")


def gather_axes(value, axes, dim):
    if not axes:
        return value
    nearer = lax.all_gather(value, axes[-1], axis=dim, tiled=True)
    return gather_axes(nearer, axes[:-1], dim)


def cut_along(value, dim, count):
    before, after = (value.shape[:dim], value.shape[dim + 1 :])
    return jnp.moveaxis(value.reshape(*before, count, -1, *after), dim, 0)


def summed_on_arrival(value, axis, dim):
    count = lax.axis_size(axis)
    blocks = lax.all_to_all(cut_along(value, dim, count), axis, 0, 0, tiled=True)
    return jnp.sum(blocks.astype(jnp.float32), axis=0)


def laid_out(blocks, dim):
    blocks = jnp.moveaxis(blocks, 0, dim)
    dims = blocks.shape
    return blocks.reshape(*dims[:dim], dims[dim] * dims[dim + 1], *dims[dim + 2 :])


def moved_by_axis(blocks, axes, order):
    inside = blocks.shape[1:]
    filled = blocks.reshape(*(lax.axis_size(a) for a in axes), *inside)
    for k in order:
        filled = lax.all_to_all(filled, axes[k], k, k, tiled=True)
    return filled.reshape(-1, *inside)


def two_step_exchange(value, groups, order, split_dim, concat_dim):
    count = lax.axis_size(groups[0]) * lax.axis_size(groups[1])
    blocks = cut_along(value, split_dim, count)
    return laid_out(moved_by_axis(blocks, groups, order), concat_dim)


def slot_table(expert_index, slot_index, kept_mask, experts):
    code = jnp.where(kept_mask > 0, expert_index * CAP + slot_index, -1)
    places = lax.broadcasted_iota(jnp.int32, (experts * CAP, code.shape[0]), 0)
    return (places == code[None, :]).astype(jnp.bfloat16)


def expert_pass(received, w_first, w_second, gather_rows, scatter_sums, send_back):
    source, slots, narrow = received.shape
    flat = received.reshape(source * slots, narrow)
    hidden_width = w_first.shape[1]

    def add_piece(total, piece, start):
        return jnp.dot(piece, w_first, preferred_element_type=jnp.float32)

    pre = gather_rows(flat, add_piece, jnp.zeros((source * slots, hidden_width), jnp.float32))
    hidden = jnp.maximum(pre, 0.0).astype(jnp.bfloat16)
    whole = jnp.dot(hidden, w_second, preferred_element_type=jnp.float32)
    summed = scatter_sums(whole)
    outgoing = summed.astype(jnp.bfloat16).reshape(source, slots, narrow)
    return send_back(outgoing)


def combine(table, returned, gate):
    flat = returned.reshape(returned.shape[0] * returned.shape[1], returned.shape[2])
    picked = lax.dot_general(
        table, flat, (((0,), (0,)), ((), ())), preferred_element_type=jnp.float32
    )
    return (gate[:, None] * picked).astype(jnp.bfloat16)


def on_device(tokens, expert_index, slot_index, kept_mask, gate_prob, w_in, w_out):
    experts = lax.axis_size(EXPERT)
    w_first = w_in[0]
    w_second = w_out[0]
    narrow = tokens.shape[2]
    tables = []
    outgoing = []
    for group in range(GROUPS):
        table = slot_table(expert_index[group], slot_index[group], kept_mask[group], experts)
        tables.append(table)
        packed = jnp.dot(table, tokens[group], preferred_element_type=jnp.float32).astype(
            jnp.bfloat16
        )
        outgoing.append(packed.reshape(experts, CAP, narrow))
    results = []
    stacked = jnp.concatenate(outgoing, axis=1)
    returned = expert_pass(
        two_step_exchange(stacked, (("expert_0", "expert_1"), "expert_2"), (1, 0), 0, 0),
        w_first,
        w_second,
        lambda flat, fold, start_value: fold(start_value, gather_axes(flat, MP, 1), jnp.int32(0)),
        lambda whole: summed_on_arrival(whole.astype(jnp.bfloat16), MP, 1),
        lambda outbound: two_step_exchange(
            outbound, (("expert_0", "expert_1"), "expert_2"), (1, 0), 0, 0
        ),
    )
    for group in range(GROUPS):
        own = returned[:, group * CAP : (group + 1) * CAP, :]
        results.append(combine(tables[group], own, gate_prob[group]))
    return jnp.stack(results)


def solution(mesh):
    torus = Mesh(
        mesh.devices.reshape(16, 2, 2, 8, 2), ("expert_0", "expert_1", "expert_2", "mp_0", "mp_1")
    )
    placed = (
        P(None, EXPERT, MP),
        P(None, EXPERT),
        P(None, EXPERT),
        P(None, EXPERT),
        P(None, EXPERT),
        P(EXPERT, None, MP),
        P(EXPERT, MP, None),
    )
    return jax.shard_map(
        on_device, mesh=torus, in_specs=placed, out_specs=P(None, EXPERT, MP), check_vma=False
    )
```

profile of v0, /device:TPU:1, one launch (start us, length us, event | category | flops | bytes accessed | tf_op | source)
XLA Modules:
  0.0 251.0 jit_solution(15718935724141948122)
XLA Ops:
  6.5 0.0 copy-start
  6.5 0.0 all-gather.2.cloned.1.call-start
  6.5 0.9 fusion.25
  7.4 1.1 convolution_convert_fusion.2
  8.6 1.1 convolution_convert_fusion.1
  9.8 0.1 pad_maximum_fusion
  9.9 0.1 copy.14
  10.0 17.6 %all_to_all.25 = bf16[32,2,1,12,128]{4,0,3,2,1:T(8,128)(2,1)S(1)} all-to-all(bf16[32,2,1,12,128]{4,0,3,2,1:T(8,128)(2,1)S(1)} %copy.14), channel_id=1, replica_groups=mesh['expert_0'=16,'expert_1'=2,'expert_2'=2,'mp_0'=8,'mp_1'=2] {'expert..., dimensions={1} | all-to-all | bytes 393216 | tf_op jit(solution)/shard_map/all_to_all | solution.py:41
  27.7 0.2 copy.15
  27.9 26.8 %all_to_all.26 = bf16[32,2,1,12,128]{4,1,3,2,0:T(2,128)(2,1)S(1)} all-to-all(bf16[32,2,1,12,128]{4,1,3,2,0:T(2,128)(2,1)S(1)} %copy.15), channel_id=1, replica_groups=mesh['expert_0'=16,'expert_1'=2,'expert_2'=2,'mp_0'=8,'mp_1'=2] {'expert..., dimensions={0} | all-to-all | bytes 393216 | tf_op jit(solution)/shard_map/all_to_all | solution.py:41
  54.8 5.3 %all_gather.6 = bf16[768,256]{1,0:T(8,128)(2,1)} all-gather(bf16[768,128]{1,0:T(8,128)(2,1)S(1)} %reshape_reshape_reshape.6), channel_id=1, replica_groups=mesh['expert_0'=16,'expert_1'=2,'expert_2'=2,'mp_0'=8,'mp_1'=2] {'mp_1'}, dimensions={1}, use_global_device_ids=true | all-gather | bytes 589824 | tf_op jit(solution)/shard_map/all_gather | solution.py:16
  60.1 0.0 all-gather.2.cloned.1.call-update
  60.2 52.6 %all-gather.2.cloned.1.call-done = bf16[768,2048]{1,0:T(8,128)(2,1)} async-done(((bf16[768,256]{1,0:T(8,128)(2,1)}), bf16[768,2048]{1,0:T(8,128)(2,1)}) %all-gather.2.cloned.1.call-update) | async-done | bytes 3145744 | tf_op jit(solution)/shard_map/all_gather | solution.py:16
  112.7 0.0 copy-done
  112.7 7.5 %fusion = bf16[96,16,8,128]{3,2,1,0:T(8,128)(2,1)} fusion(bf16[1,384,2048]{2,1,0:T(8,128)(2,1)S(1)} %copy-done, bf16[768,2048]{1,0:T(8,128)(2,1)} %all-gather.2.cloned.1.call-done, bf16[1,2048,384]{2,1,0:T(8,128)(2,1)} %param.12), kind=kOutput, calls=%fused_computation.2 | convolution fusion | flops 2418081792 | bytes 9437184 | tf_op jit(solution)/shard_map/dot_general | solution.py:67
  120.2 2.7 %copy.25 = bf16[96,16,8,128]{3,2,0,1:T(8,128)(2,1)S(1)} copy(bf16[96,16,8,128]{3,2,1,0:T(8,128)(2,1)} %fusion) | data formatting | bytes 6291456 | tf_op jit(solution)/shard_map/reshape | solution.py:22
  122.9 70.8 %all_to_all.27 = bf16[16,768,128]{2,1,0:T(8,128)(2,1)} all-to-all(bf16[16,768,128]{2,1,0:T(8,128)(2,1)S(1)} %bitcast.36), channel_id=1, replica_groups=mesh['expert_0'=16,'expert_1'=2,'expert_2'=2,'mp_0'=8,'mp_1'=2] {'mp_0',..., dimensions={0} | all-to-all | bytes 6291456 | tf_op jit(solution)/shard_map/all_to_all | solution.py:27
  193.7 2.4 reduce_sum.12
  196.1 0.0 copy-start.1
  196.1 0.1 copy.18
  196.2 11.7 %all_to_all.28 = bf16[32,2,1,12,128]{4,0,3,2,1:T(8,128)(2,1)S(1)} all-to-all(bf16[32,2,1,12,128]{4,0,3,2,1:T(8,128)(2,1)S(1)} %copy.18), channel_id=1, replica_groups=mesh['expert_0'=16,'expert_1'=2,'expert_2'=2,'mp_0'=8,'mp_1'=2] {'expert..., dimensions={1} | all-to-all | bytes 393216 | tf_op jit(solution)/shard_map/all_to_all | solution.py:41
  207.9 0.9 copy.19
  208.8 15.1 %all-to-all-start.4 = ((bf16[32,2,1,12,128]{4,1,3,2,0:T(2,128)(2,1)}), bf16[32,2,1,12,128]{4,1,3,2,0:T(2,128)(2,1)S(1)}, u32[]{:S(2)}, u32[]{:S(2)}) async-start(bf16[32,2,1,12,128]{4,1,3,2,0:T(2,128)(2,1)} %copy.19), calls=%async_computation.4 | async-start | bytes 393216 | tf_op jit(solution)/shard_map/all_to_all | solution.py:41
  223.9 0.0 copy-done.1
  224.0 18.3 %all-to-all-done.4 = bf16[32,2,1,12,128]{4,1,3,2,0:T(2,128)(2,1)S(1)} async-done(((bf16[32,2,1,12,128]{4,1,3,2,0:T(2,128)(2,1)}), bf16[32,2,1,12,128]{4,1,3,2,0:T(2,128)(2,1)S(1)}, u32[]{:S(2)}, u32[]{:S(2)}) %all-to-all-start.4) | async-done | bytes 196640 | tf_op jit(solution)/shard_map/all_to_all | solution.py:41
  242.3 0.2 copy.20
  242.5 0.1 copy.21
  242.6 0.1 copy.22
  242.7 0.4 fusion.13
  243.1 0.4 fusion.12
  243.4 0.7 pad_maximum_fusion.1
  (9 shorter events, 0.3 us)
Async XLA Ops:
  6.5 106.2 %copy-start = (bf16[1,384,2048]{2,1,0:T(8,128)(2,1)S(1)}, bf16[1,384,2048]{2,1,0:T(8,128)(2,1)}, u32[]{:S(2)}) copy-start(bf16[1,384,2048]{2,1,0:T(8,128)(2,1)} %param.13) | copy-start | bytes 4718596
  6.5 106.2 %all-gather.2.cloned.1.call-start = ((), (), s32[]{:S(2)}) async-start(), calls=%async_computation.5 | async-start | bytes 3538944 | tf_op jit(solution)/shard_map/all_gather | solution.py:16
  196.1 27.9 %copy-start.1 = (f32[2,320]{1,0:T(2,128)S(1)}, f32[2,320]{1,0:T(2,128)}, u32[]{:S(2)}) copy-start(f32[2,320]{1,0:T(2,128)} %param.11) | copy-start | bytes 7684
  208.8 33.5 %all-to-all-start.4 = ((bf16[32,2,1,12,128]{4,1,3,2,0:T(2,128)(2,1)}), bf16[32,2,1,12,128]{4,1,3,2,0:T(2,128)(2,1)S(1)}, u32[]{:S(2)}, u32[]{:S(2)}) async-start(bf16[32,2,1,12,128]{4,1,3,2,0:T(2,128)(2,1)} %copy.19), calls=%async_computation.4 | async-start | bytes 393216 | tf_op jit(solution)/shard_map/all_to_all | solution.py:41
Sparse Core Ops, SparseCore 0:
  60.3 52.4 all-gather.1
where the time goes:
time: 252 us; the launch traced here: 251 us
  blocking collectives  132 us (52%)
  waiting for transfers between devices  70.9 us (28%)
  starting transfers between devices  15.1 us (6%)
  between operations  13.6 us (5%)
  matrix products  10.5 us (4%)
  local copies, waits for them, and re-layouts  4.57 us (2%)
  other arithmetic  4.05 us (2%)
    all_to_all x1, blocking collectives, summed_on_arrival(): lax.all_to_all(cut_along(value, dim, count), axis, 0, 0, tiled=True)  70.8 us
    all_to_all x3, blocking collectives, moved_by_axis(): filled = lax.all_to_all(filled, axes[k], k, k, tiled=True)  56.2 us
    all_gather x1, waiting for transfers between devices, gather_axes(): nearer = lax.all_gather(value, axes[-1], axis=dim, tiled=True)  52.6 us
    all_to_all x1, waiting for transfers between devices, moved_by_axis(): filled = lax.all_to_all(filled, axes[k], k, k, tiled=True)  18.3 us
    all_to_all x1, starting transfers between devices, moved_by_axis(): filled = lax.all_to_all(filled, axes[k], k, k, tiled=True)  15.1 us
    dot_general x1, matrix products, expert_pass(): whole = jnp.dot(hidden, w_second, preferred_element_type=jnp.float32)  7.47 us
    all_gather x1, blocking collectives, gather_axes(): nearer = lax.all_gather(value, axes[-1], axis=dim, tiled=True)  5.32 us
  transfers between devices with their start and end apart: 2, of which 2 were waited for; matrix products, arithmetic and copies ran while one was open for 0% of the time, Pallas kernels for 0%

commit v1 on v0

v1 whole, which is shorter than its diff:
```python
import jax
import jax.numpy as jnp
from jax import lax
from jax.experimental import pallas as pl
from jax.experimental.pallas import tpu as pltpu
from jax.sharding import Mesh
from jax.sharding import PartitionSpec as P

GROUPS = 2
CAP = 6
EXPERT = ("expert_0", "expert_1", "expert_2")
MP = ("mp_0", "mp_1")
MESH = pl.DeviceIdType.MESH
NY = 8
HALF = NY // 2
PLUS, MINUS = 0, 1


def cut_along(value, dim, count):
    before, after = (value.shape[:dim], value.shape[dim + 1 :])
    return jnp.moveaxis(value.reshape(*before, count, -1, *after), dim, 0)


def laid_out(blocks, dim):
    blocks = jnp.moveaxis(blocks, 0, dim)
    dims = blocks.shape
    return blocks.reshape(*dims[:dim], dims[dim] * dims[dim + 1], *dims[dim + 2 :])


def moved_by_axis(blocks, axes, order):
    inside = blocks.shape[1:]
    filled = blocks.reshape(*(lax.axis_size(a) for a in axes), *inside)
    for k in order:
        filled = lax.all_to_all(filled, axes[k], k, k, tiled=True)
    return filled.reshape(-1, *inside)


def two_step_exchange(value, groups, order, split_dim, concat_dim):
    count = lax.axis_size(groups[0]) * lax.axis_size(groups[1])
    blocks = cut_along(value, split_dim, count)
    return laid_out(moved_by_axis(blocks, groups, order), concat_dim)


def slot_table(expert_index, slot_index, kept_mask, experts):
    code = jnp.where(kept_mask > 0, expert_index * CAP + slot_index, -1)
    places = lax.broadcasted_iota(jnp.int32, (experts * CAP, code.shape[0]), 0)
    return (places == code[None, :]).astype(jnp.bfloat16)


GATHER = ((0, 1), (0, 0), (1, 0))
REDUCE = ((1, 0), (0, 0), (0, 1))


def row_range(piece, direction, distance, rows):
    column, half = piece
    start, size = half * (rows // 2), rows // 2
    if distance < HALF:
        return start, size
    if piece == (0, 0):
        return (start, size) if direction == PLUS else None
    if piece == (0, 1):
        return (start, size) if direction == MINUS else None
    part = size // 2
    return (start, part) if direction == PLUS else (start + part, size - part)


def expert_kernel(
    x_ref, win_hbm, wout_hbm, out_ref,
    win, wout, load_sem, gath, pre, hidden,
    gy_send, gy_recv, gx_send, gx_recv,
    ry_buf, ry_out, rx_buf, rx_out,
    ry_send, ry_recv, rx_send, rx_recv,
):
    rows, width = x_ref.shape
    half = rows // 2
    y = lax.axis_index("mp_0")
    c = lax.axis_index("mp_1")
    up = lax.rem(y + 1, NY)
    down = lax.rem(y + NY - 1, NY)
    ring = ({"mp_0": up}, {"mp_0": down})
    across = {"mp_1": 1 - c}

    first = pltpu.make_async_copy(win_hbm.at[0], win, load_sem.at[0])
    second = pltpu.make_async_copy(wout_hbm.at[0], wout, load_sem.at[1])
    first.start()
    second.start()

    barrier = pltpu.get_barrier_semaphore()
    for device in (ring[0], ring[1], across):
        pl.semaphore_signal(barrier, inc=1, device_id=device, device_id_type=MESH)
    pl.semaphore_wait(barrier, 3)

    def feature(r, column):
        place = lax.rem(y + r, NY) * 2 + (c if column == 0 else 1 - c)
        return pl.ds(pl.multiple_of(place * width, width), width)

    sent = []

    def push(src, dst, send_sem, recv_sem, device):
        copy = pltpu.make_async_remote_copy(
            src_ref=src, dst_ref=dst, send_sem=send_sem, recv_sem=recv_sem,
            device_id=device, device_id_type=MESH,
        )
        copy.start()
        sent.append(copy)

    def arrived(dst, recv_sem, send_sem):
        pltpu.make_async_remote_copy(
            src_ref=dst, dst_ref=dst, send_sem=send_sem, recv_sem=recv_sem,
            device_id=across, device_id_type=MESH,
        ).wait_recv()

    def held(r, column, start, size):
        if r == 0 and column == 0:
            return x_ref.at[pl.ds(start, size)]
        return gath.at[r, column, pl.ds(start, size)]

    def ring_slot(direction, distance):
        return (NY - distance) if direction == PLUS else distance

    def gather_send(direction, distance, p):
        span = row_range(GATHER[p], direction, distance, rows)
        if span is None:
            return
        column = GATHER[p][0]
        here = 0 if distance == 1 else ring_slot(direction, distance - 1)
        there = ring_slot(direction, distance)
        push(
            held(here, column, *span),
            gath.at[there, column, pl.ds(*span)],
            gy_send.at[direction, distance - 1, p],
            gy_recv.at[direction, distance - 1, p],
            ring[direction],
        )

    def cross_send(r):
        push(
            held(r, 0, half, half), gath.at[r, 1, pl.ds(half, half)],
            gx_send.at[r], gx_recv.at[r], across,
        )

    def cross_wait(r):
        arrived(gath.at[r, 1, pl.ds(half, half)], gx_recv.at[r], gx_send.at[r])

    def fold(r, column, start, size, first_time=False):
        piece = held(r, column, start, size)[...]
        part = jnp.dot(piece, win[feature(r, column), :], preferred_element_type=jnp.float32)
        if first_time:
            pre[pl.ds(start, size), :] = part
        else:
            pre[pl.ds(start, size), :] += part

    push(
        held(0, 0, 0, half), gath.at[0, 1, pl.ds(0, half)],
        gx_send.at[NY], gx_recv.at[NY], across,
    )
    for p in (0, 1):
        gather_send(PLUS, 1, p)
        gather_send(MINUS, 1, p)
    cross_send(0)
    first.wait()
    fold(0, 0, 0, half, True)
    arrived(gath.at[0, 1, pl.ds(0, half)], gx_recv.at[NY], gx_send.at[NY])
    gather_send(PLUS, 1, 2)
    gather_send(MINUS, 1, 2)
    fold(0, 0, half, half, True)
    fold(0, 1, 0, half)
    for distance in range(1, HALF + 1):
        for p in range(3):
            column, part_half = GATHER[p]
            for direction in (PLUS, MINUS):
                span = row_range(GATHER[p], direction, distance, rows)
                if span is None:
                    continue
                r = ring_slot(direction, distance)
                arrived(
                    gath.at[r, column, pl.ds(*span)],
                    gy_recv.at[direction, distance - 1, p],
                    gy_send.at[direction, distance - 1, p],
                )
                if distance < HALF:
                    gather_send(direction, distance + 1, p)
                if (column, part_half) == (0, 1):
                    cross_send(r)
                fold(r, column, *span)
        for r in ((0,) if distance == 1 else (NY - distance + 1, distance - 1)):
            cross_wait(r)
            fold(r, 1, half, half)
    cross_wait(HALF)
    fold(HALF, 1, half, half)
    for copy in sent:
        copy.wait_send()
    sent.clear()

    hidden[...] = jnp.maximum(pre[...], 0.0).astype(jnp.bfloat16)
    second.wait()

    def block(r, column, start, size):
        return jnp.dot(
            hidden[pl.ds(start, size), :], wout[:, feature(r, column)],
            preferred_element_type=jnp.float32,
        )

    def cross_term(r):
        rx_out[r] = block(r, 1, half, half).astype(jnp.bfloat16)
        push(rx_out.at[r], rx_buf.at[r], rx_send.at[r], rx_recv.at[r], across)

    def cross_arrived(r):
        arrived(rx_buf.at[r], rx_recv.at[r], rx_send.at[r])

    def ring_arrived(direction, distance, p, span):
        slot = ry_buf.at[direction, distance, p, pl.ds(span[0] % half, span[1])]
        arrived(slot, ry_recv.at[direction, distance, p], ry_send.at[direction, distance, p])
        return slot

    def reduce_send(direction, distance, p):
        piece = REDUCE[p]
        r = distance if direction == PLUS else NY - distance
        full = row_range(piece, direction, distance, rows)
        if full is None:
            return
        total = block(r, piece[0], *full)
        if piece == (0, 1):
            total = total + rx_buf[r].astype(jnp.float32)
        out = ry_out.at[direction, distance - 1, p, pl.ds(full[0] % half, full[1])]
        if distance < HALF:
            coming = row_range(piece, direction, distance + 1, rows)
            if coming is not None:
                slot = ring_arrived(direction, distance, p, coming)
                if coming == full:
                    total = total + slot[...].astype(jnp.float32)
                else:
                    low = coming[0] - full[0]
                    parts = []
                    if low > 0:
                        parts.append(total[:low])
                    parts.append(total[low : low + coming[1]] + slot[...].astype(jnp.float32))
                    if low + coming[1] < full[1]:
                        parts.append(total[low + coming[1] :])
                    total = jnp.concatenate(parts, axis=0)
        out[...] = total.astype(jnp.bfloat16)
        push(
            out, ry_buf.at[direction, distance - 1, p, pl.ds(full[0] % half, full[1])],
            ry_send.at[direction, distance - 1, p], ry_recv.at[direction, distance - 1, p],
            ring[direction],
        )

    cross_term(HALF)
    for p in (0, 1):
        reduce_send(PLUS, HALF, p)
        reduce_send(MINUS, HALF, p)
    cross_term(HALF - 1)
    cross_term(HALF + 1)
    cross_arrived(HALF)
    reduce_send(MINUS, HALF, 2)
    for distance in range(HALF - 1, 0, -1):
        for r in ((distance - 1, NY - distance + 1) if distance > 1 else (0,)):
            cross_term(r)
        for p in range(3):
            if p == 2:
                cross_arrived(distance)
                cross_arrived(NY - distance)
            for direction in (PLUS, MINUS):
                reduce_send(direction, distance, p)

    def last(p):
        piece = REDUCE[p]
        start = piece[1] * half
        total = block(0, piece[0], start, half)
        for direction in (PLUS, MINUS):
            total = total + ring_arrived(direction, 0, p, (start, half))[...].astype(jnp.float32)
        return total

    rx_out[NY] = last(0).astype(jnp.bfloat16)
    push(rx_out.at[NY], rx_buf.at[NY], rx_send.at[NY], rx_recv.at[NY], across)
    upper = last(1)
    cross_arrived(0)
    lower = last(2) + rx_buf[0].astype(jnp.float32)
    out_ref[pl.ds(half, half), :] = lower.astype(jnp.bfloat16)
    cross_arrived(NY)
    out_ref[pl.ds(0, half), :] = (upper + rx_buf[NY].astype(jnp.float32)).astype(jnp.bfloat16)
    for copy in sent:
        copy.wait_send()


def expert_pass(x, w_in, w_out):
    rows, width = x.shape
    half = rows // 2
    bf16, f32 = jnp.bfloat16, jnp.float32
    dma = pltpu.SemaphoreType.DMA
    return pl.pallas_call(
        expert_kernel,
        out_shape=jax.ShapeDtypeStruct((rows, width), bf16),
        in_specs=[
            pl.BlockSpec(memory_space=pltpu.VMEM),
            pl.BlockSpec(memory_space=pl.ANY),
            pl.BlockSpec(memory_space=pl.ANY),
        ],
        out_specs=pl.BlockSpec(memory_space=pltpu.VMEM),
        scratch_shapes=[
            pltpu.VMEM(w_in.shape[1:], bf16),
            pltpu.VMEM(w_out.shape[1:], bf16),
            dma((2,)),
            pltpu.VMEM((NY, 2, rows, width), bf16),
            pltpu.VMEM((rows, w_in.shape[2]), f32),
            pltpu.VMEM((rows, w_in.shape[2]), bf16),
            dma((2, HALF, 3)), dma((2, HALF, 3)), dma((NY + 1,)), dma((NY + 1,)),
            pltpu.VMEM((2, HALF, 3, half, width), bf16),
            pltpu.VMEM((2, HALF, 3, half, width), bf16),
            pltpu.VMEM((NY + 1, half, width), bf16),
            pltpu.VMEM((NY + 1, half, width), bf16),
            dma((2, HALF, 3)), dma((2, HALF, 3)), dma((NY + 1,)), dma((NY + 1,)),
        ],
        compiler_params=pltpu.CompilerParams(
            collective_id=0, has_side_effects=True, vmem_limit_bytes=48 * 1024 * 1024
        ),
        name="expert_ring",
    )(x, w_in, w_out)


def combine(table, returned, gate):
    flat = returned.reshape(returned.shape[0] * returned.shape[1], returned.shape[2])
    picked = lax.dot_general(
        table, flat, (((0,), (0,)), ((), ())), preferred_element_type=jnp.float32
    )
    return (gate[:, None] * picked).astype(jnp.bfloat16)


def on_device(tokens, expert_index, slot_index, kept_mask, gate_prob, w_in, w_out):
    experts = lax.axis_size(EXPERT)
    narrow = tokens.shape[2]
    tables = []
    outgoing = []
    for group in range(GROUPS):
        table = slot_table(expert_index[group], slot_index[group], kept_mask[group], experts)
        tables.append(table)
        packed = jnp.dot(table, tokens[group], preferred_element_type=jnp.float32).astype(
            jnp.bfloat16
        )
        outgoing.append(packed.reshape(experts, CAP, narrow))
    results = []
    stacked = jnp.concatenate(outgoing, axis=1)
    split = (("expert_0", "expert_1"), "expert_2")
    received = two_step_exchange(stacked, split, (1, 0), 0, 0)
    source, slots, _ = received.shape
    summed = expert_pass(received.reshape(source * slots, narrow), w_in, w_out)
    returned = two_step_exchange(summed.reshape(source, slots, narrow), split, (1, 0), 0, 0)
    for group in range(GROUPS):
        own = returned[:, group * CAP : (group + 1) * CAP, :]
        results.append(combine(tables[group], own, gate_prob[group]))
    return jnp.stack(results)


def solution(mesh):
    torus = Mesh(
        mesh.devices.reshape(16, 2, 2, 8, 2), ("expert_0", "expert_1", "expert_2", "mp_0", "mp_1")
    )
    placed = (
        P(None, EXPERT, MP),
        P(None, EXPERT),
        P(None, EXPERT),
        P(None, EXPERT),
        P(None, EXPERT),
        P(EXPERT, None, MP),
        P(EXPERT, MP, None),
    )
    return jax.shard_map(
        on_device, mesh=torus, in_specs=placed, out_specs=P(None, EXPERT, MP), check_vma=False
    )
```

time: 252 us -> 142 us (0.56)
  blocking collectives: 132 us -> 55.1 us
  Pallas kernels: 0 us -> 53.7 us
  waiting for transfers between devices: 70.9 us -> 18.3 us
  between operations: 13.6 us -> 0.19 us
  starting transfers between devices: 15.1 us -> 5.69 us
  matrix products: 10.5 us -> 2.98 us
    all_to_all x1 -> x0, blocking collectives: 70.8 us -> none  [summed_on_arrival(): lax.all_to_all(cut_along(value, dim, count), axis, 0, 0, tiled=True)]
    pallas_call x0 -> x1, Pallas kernels: none -> 53.7 us  [expert_pass(): pl.pallas_call(expert_kernel, out_shape=jax.ShapeDtypeStruct((rows, width...]
    all_gather x1 -> x0, waiting for transfers between devices: 52.6 us -> none  [gather_axes(): nearer = lax.all_gather(value, axes[-1], axis=dim, tiled=True)]
    all_to_all x1, starting transfers between devices: 15.1 us -> 5.69 us  [moved_by_axis(): filled = lax.all_to_all(filled, axes[k], k, k, tiled=True)]
    dot_general x1 -> x0, matrix products: 7.47 us -> none  [expert_pass(): whole = jnp.dot(hidden, w_second, preferred_element_type=jnp.float32)]
    all_gather x1 -> x0, blocking collectives: 5.32 us -> none  [gather_axes(): nearer = lax.all_gather(value, axes[-1], axis=dim, tiled=True)]
    reshape x1 -> x0, local copies, waits for them, and re-layouts: 2.69 us -> none  [cut_along(): return jnp.moveaxis(value.reshape(*before, count, -1, *after), dim, 0)]
  transfers between devices with their start and end apart: 2 -> 1, of which waited for: 2 -> 1; matrix products, arithmetic and copies ran while one was open for 0% -> 0% of each run, Pallas kernels for 0% -> 0%
where the time goes in v1:
time: 142 us; the launch traced here: 141 us
  blocking collectives  55.1 us (39%)
  Pallas kernels  53.7 us (38%)
  waiting for transfers between devices  18.3 us (13%)
  starting transfers between devices  5.69 us (4%)
  local copies, waits for them, and re-layouts  3.52 us (2%)
  matrix products  2.98 us (2%)
  other arithmetic  1.57 us (1%)
    all_to_all x3, blocking collectives, moved_by_axis(): filled = lax.all_to_all(filled, axes[k], k, k, tiled=True)  55.1 us
    pallas_call x1, Pallas kernels, expert_pass(): pl.pallas_call(expert_kernel, out_shape=jax.ShapeDtypeStruct((rows, width...  53.7 us
    all_to_all x1, waiting for transfers between devices, moved_by_axis(): filled = lax.all_to_all(filled, axes[k], k, k, tiled=True)  18.3 us
    all_to_all x1, starting transfers between devices, moved_by_axis(): filled = lax.all_to_all(filled, axes[k], k, k, tiled=True)  5.69 us
  transfers between devices with their start and end apart: 1, of which 1 were waited for; matrix products, arithmetic and copies ran while one was open for 0% of the time, Pallas kernels for 0%

profile of v1, /device:TPU:1, one launch (start us, length us, event | category | flops | bytes accessed | tf_op | source)
XLA Modules:
  0.0 141.1 jit_solution(12284571369354016508)
XLA Ops:
  0.0 0.8 fusion.12
  0.8 1.1 convolution_convert_fusion.1
  2.0 1.1 convolution_convert_fusion
  3.1 0.0 copy-start.1
  3.2 0.0 copy-start
  3.2 0.1 pad_maximum_fusion
  3.3 0.1 copy.13
  3.4 17.8 %all_to_all.20 = bf16[32,2,1,12,128]{4,0,3,2,1:T(8,128)(2,1)S(1)} all-to-all(bf16[32,2,1,12,128]{4,0,3,2,1:T(8,128)(2,1)S(1)} %copy.13), channel_id=1, replica_groups=mesh['expert_0'=16,'expert_1'=2,'expert_2'=2,'mp_0'=8,'mp_1'=2] {'expert..., dimensions={1} | all-to-all | bytes 393216 | tf_op jit(solution)/shard_map/all_to_all | solution.py:34
  21.2 0.2 copy.14
  21.4 26.8 %all_to_all.21 = bf16[32,2,1,12,128]{4,1,3,2,0:T(2,128)(2,1)S(1)} all-to-all(bf16[32,2,1,12,128]{4,1,3,2,0:T(2,128)(2,1)S(1)} %copy.14), channel_id=1, replica_groups=mesh['expert_0'=16,'expert_1'=2,'expert_2'=2,'mp_0'=8,'mp_1'=2] {'expert..., dimensions={0} | all-to-all | bytes 393216 | tf_op jit(solution)/shard_map/all_to_all | solution.py:34
  48.2 0.7 copy.15
  48.9 1.0 reshape_reshape_reshape.6.x_ref
  49.9 0.0 copy-done.1
  50.0 0.0 copy-done
  50.0 53.7 %expert_ring.1 = bf16[768,128]{1,0:T(8,128)(2,1)S(1)} custom-call(bf16[768,128]{1,0:T(8,128)(2,1)S(1)} %reshape_reshape_reshape.6.x_ref, bf16[1,2048,384]{2,1,0:T(8,128)(2,1)S(1)} %copy-done, bf16[1,384,2048]{2,1,0:T(8,128)(2,1)S(1)} %copy-done.1), custom_call_target="tpu_custom_call" | custom-call | tf_op jit(solution)/shard_map/expert_ring/pallas_call | solution.py:291
  103.7 0.0 copy-start.2
  103.8 0.1 copy.16
  103.9 10.5 %all_to_all.22 = bf16[32,2,1,12,128]{4,0,3,2,1:T(8,128)(2,1)S(1)} all-to-all(bf16[32,2,1,12,128]{4,0,3,2,1:T(8,128)(2,1)S(1)} %copy.16), channel_id=1, replica_groups=mesh['expert_0'=16,'expert_1'=2,'expert_2'=2,'mp_0'=8,'mp_1'=2] {'expert..., dimensions={1} | all-to-all | bytes 393216 | tf_op jit(solution)/shard_map/all_to_all | solution.py:34
  114.4 0.9 copy.17
  115.2 5.7 %all-to-all-start.3 = ((bf16[32,2,1,12,128]{4,1,3,2,0:T(2,128)(2,1)}), bf16[32,2,1,12,128]{4,1,3,2,0:T(2,128)(2,1)S(1)}, u32[]{:S(2)}, u32[]{:S(2)}) async-start(bf16[32,2,1,12,128]{4,1,3,2,0:T(2,128)(2,1)} %copy.17), calls=%async_computation.3 | async-start | bytes 393216 | tf_op jit(solution)/shard_map/all_to_all | solution.py:34
  120.9 0.0 copy-done.2
  121.0 18.3 %all-to-all-done.3 = bf16[32,2,1,12,128]{4,1,3,2,0:T(2,128)(2,1)S(1)} async-done(((bf16[32,2,1,12,128]{4,1,3,2,0:T(2,128)(2,1)}), bf16[32,2,1,12,128]{4,1,3,2,0:T(2,128)(2,1)S(1)}, u32[]{:S(2)}, u32[]{:S(2)}) %all-to-all-start.3) | async-done | bytes 196640 | tf_op jit(solution)/shard_map/all_to_all | solution.py:34
  139.3 0.2 copy.18
  139.5 0.1 copy.19
  139.6 0.1 copy.20
  139.7 0.4 fusion.3
  140.1 0.4 fusion.2
  140.4 0.7 pad_maximum_fusion.1
  (7 shorter events, 0.2 us)
Async XLA Ops:
  3.1 46.8 %copy-start.1 = (bf16[1,384,2048]{2,1,0:T(8,128)(2,1)S(1)}, bf16[1,384,2048]{2,1,0:T(8,128)(2,1)}, u32[]{:S(2)}) copy-start(bf16[1,384,2048]{2,1,0:T(8,128)(2,1)} %wout_hbm.1) | copy-start | bytes 4718596
  3.2 46.8 %copy-start = (bf16[1,2048,384]{2,1,0:T(8,128)(2,1)S(1)}, bf16[1,2048,384]{2,1,0:T(8,128)(2,1)}, u32[]{:S(2)}) copy-start(bf16[1,2048,384]{2,1,0:T(8,128)(2,1)} %win_hbm.1) | copy-start | bytes 4718596
  103.7 17.2 %copy-start.2 = (f32[2,320]{1,0:T(2,128)S(1)}, f32[2,320]{1,0:T(2,128)}, u32[]{:S(2)}) copy-start(f32[2,320]{1,0:T(2,128)} %param.11) | copy-start | bytes 7684
  115.2 24.0 %all-to-all-start.3 = ((bf16[32,2,1,12,128]{4,1,3,2,0:T(2,128)(2,1)}), bf16[32,2,1,12,128]{4,1,3,2,0:T(2,128)(2,1)S(1)}, u32[]{:S(2)}, u32[]{:S(2)}) async-start(bf16[32,2,1,12,128]{4,1,3,2,0:T(2,128)(2,1)} %copy.17), calls=%async_computation.3 | async-start | bytes 393216 | tf_op jit(solution)/shard_map/all_to_all | solution.py:34
